TPU v7x, 256 devices: a 8x8x2 block of a 8x8x16 slice. The times are simulated.
256 devices in a mesh: cosmo: 2 (over z), row: 128 (over y, x, core).
Axes of the slice: x: 8, y: 8, z: 2, core: 2. Of those that a mesh axis runs over, the one named last changes fastest.
The devices are a block of a 8x8x16 slice.
Arguments:
- potentials: float32 [4, 2048, 16384], P('cosmo', 'row'), parts along dimension 0, may hold values from -3 to 3
- ratios: float32 [6], P('cosmo'), parts along dimension 0, may hold values from 0.3 to 0.9
- row_offset: int32 [256], P('cosmo'), parts along dimension 0, may hold values from 0 to 7
- col_offset: int32 [256], P('cosmo'), parts along dimension 0, may hold values from 0 to 127
Outputs:
- convergence: float32 [4096, 16384], P(('cosmo', 'row')), parts along dimension 0
- shear_map: float32 [2, 4096, 16384], P(None, ('cosmo', 'row')), parts along dimension 1
- rotation: float32 [4096, 16384], P(('cosmo', 'row')), parts along dimension 0
- displacement: float32 [2, 4096, 16384], P(None, ('cosmo', 'row')), parts along dimension 1
There are 2 independent parts, one for each index of `cosmo`. A program takes and returns all parts, laid end to end along the dimension named above; each array names one. Nothing has to cross between parts.
Inputs may be any that keep to these rules, and one draw needn't show every extreme that they name: `row_offset`: row offsets count blocks of 256 rows.
All inputs are finite; a program needn't handle non-finite values.
Results may differ from a plain program's by a relative error of at most 0.00002.
Values sent between devices are 32-bit elements; how exact they have to be, the bound alone decides.
No kernel may reach another device: no remote copies, remote signals or barrier semaphores. Data moves between devices by JAX's collectives and lax.ppermute only.
A program may use at most 128 MiB of HBM per device.

v0:
```python
import jax
import jax.numpy as jnp
from jax import lax
from jax.sharding import PartitionSpec as P

BITS = 3
RB = 8


def with_halo(cells, sides, width):
    for axis, dim in sides:
        count = lax.axis_size(axis)
        head = lax.slice_in_dim(cells, 0, width, axis=dim)
        tail = lax.slice_in_dim(cells, cells.shape[dim] - width, cells.shape[dim], axis=dim)
        cells = jnp.concatenate(
            [
                lax.ppermute(tail, axis, [(i, (i + 1) % count) for i in range(count)]),
                cells,
                lax.ppermute(head, axis, [((i + 1) % count, i) for i in range(count)]),
            ],
            axis=dim,
        )
    return cells


def passed_along(x, axis, by):
    size = lax.axis_size(axis)
    return lax.ppermute(x, axis, [(i, (i + by) % size) for i in range(size)])


def column_slope(field):
    return (
        8.0 * (jnp.roll(field, -1, 2) - jnp.roll(field, 1, 2))
        - (jnp.roll(field, -2, 2) - jnp.roll(field, 2, 2))
    ) / 12.0


def row_slope(padded, height):
    return (
        8.0 * (padded[:, 3 : height + 3] - padded[:, 1 : height + 1])
        - (padded[:, 4 : height + 4] - padded[:, 0:height])
    ) / 12.0


def derive(field):
    height = field.shape[1]
    padded = with_halo(field, (("row", 1),), 4)
    widened = row_slope(padded, height + 4)
    slope_r = widened[:, 2 : height + 2]
    curve_rr = row_slope(widened, height)
    slope_c = column_slope(field)
    return (slope_r, slope_c, curve_rr, column_slope(slope_r), column_slope(slope_c))


def assemble(nearer, farther, ratios):
    near_r, near_c, near_rr, near_rc, near_cc = nearer
    far_r, far_c, far_rr, far_rc, far_cc = farther
    beta_near = ratios[0]
    beta_one = ratios[1]
    beta_two = ratios[2]
    inner_rr = 1.0 - beta_near * near_rr
    inner_rc = -beta_near * near_rc
    inner_cc = 1.0 - beta_near * near_cc
    chain_rr = far_rr * inner_rr + far_rc * inner_rc
    chain_rc = far_rr * inner_rc + far_rc * inner_cc
    chain_cr = far_rc * inner_rr + far_cc * inner_rc
    chain_cc = far_rc * inner_rc + far_cc * inner_cc
    total_rr = 1.0 - beta_one * near_rr - beta_two * chain_rr
    total_rc = -beta_one * near_rc - beta_two * chain_rc
    total_cr = -beta_one * near_rc - beta_two * chain_cr
    total_cc = 1.0 - beta_one * near_cc - beta_two * chain_cc
    convergence = 1.0 - 0.5 * (total_rr + total_cc)
    shear_map = jnp.stack([0.5 * (total_rr - total_cc), -0.5 * (total_rc + total_cr)])
    rotation = 0.5 * (total_rc - total_cr)
    displacement = jnp.stack(
        [beta_one * near_r + beta_two * far_r, beta_one * near_c + beta_two * far_c]
    )
    return (convergence, shear_map, rotation, displacement)


def per_device(potentials, ratios, row_offset, col_offset):
    devices = lax.axis_size("row")
    height = potentials.shape[1]
    columns = potentials.shape[2]
    blocks = columns // 128
    source = (jnp.arange(blocks, dtype=jnp.int32) + col_offset) % blocks
    stride = devices // RB
    fields = derive(potentials[0:1])
    nearer = tuple((member[0] for member in fields))
    strips = potentials[1].reshape(height, blocks, 128)
    left_part = jnp.take(strips, (source - 1) % blocks, axis=1)[:, :, 64:]
    middle_part = jnp.take(strips, source, axis=1)
    right_part = jnp.take(strips, (source + 1) % blocks, axis=1)[:, :, :64]
    windows = jnp.concatenate([left_part, middle_part, right_part], axis=2)
    for bit_level in range(BITS):
        arrived = passed_along(windows, "row", devices - stride * 2**bit_level)
        picked = (row_offset // 2**bit_level % 2 == 1).reshape(1, blocks, 1)
        windows = jnp.where(picked, arrived, windows)
    derived = derive(windows.reshape(1, height, blocks * 256))
    farther = tuple(
        (
            member[0].reshape(height, blocks, 256)[:, :, 64:192].reshape(height, columns)
            for member in derived
        )
    )
    return assemble(nearer, farther, ratios)


def solution(mesh):
    return jax.shard_map(
        per_device,
        mesh=mesh,
        in_specs=(P("cosmo", "row", None), P("cosmo"), P("cosmo"), P("cosmo")),
        out_specs=(
            P(("cosmo", "row"), None),
            P(None, ("cosmo", "row"), None),
            P(("cosmo", "row"), None),
            P(None, ("cosmo", "row"), None),
        ),
        check_vma=False,
    )
```

profile of v0, /device:TPU:543, one launch (start us, length us, event | category | flops | bytes accessed | tf_op | source)
XLA Modules:
  0.0 413.0 jit_solution(15362464744143215431)
XLA Ops:
  0.6 0.7 compare_and_fusion.2
  1.4 1.7 fusion.72
  3.9 0.8 gather_fusion.2
  4.6 1.7 gather_fusion.1
  6.4 1.7 gather_fusion
  8.1 1.5 select_bitcast_fusion.2
  10.9 2.2 pad_maximum_fusion.1
  13.2 0.9 fusion.71
  14.1 1.8 collective-permute-start
  15.9 1.7 fusion.67
  17.6 1.7 fusion.69
  19.3 0.6 fusion.90
  22.4 1.8 collective-permute-done.1
  24.2 1.2 pad_maximum_fusion.4
  25.4 1.7 fusion.17
  27.3 36.8 %collective-permute-done.2 = f32[16,128,256]{2,0,1:T(8,128)} collective-permute-done((f32[16,128,256]{2,0,1:T(8,128)}, f32[16,128,256]{2,0,1:T(8,128)}, u32[]{:S(2)}, u32[]{:S(2)}) %collective-permute-start.2) | collective-permute-done | bytes 2097184 | tf_op jit(solution)/shard_map/ppermute | solution.py:28
  64.2 2.6 broadcast_select_fusion
  66.8 10.3 %collective-permute-start.3 = (f32[16,128,256]{2,0,1:T(8,128)S(1)}, f32[16,128,256]{2,0,1:T(8,128)S(1)}, u32[]{:S(2)}, u32[]{:S(2)}) collective-permute-start(f32[16,128,256]{2,0,1:T(8,128)S(1)} %broadcast_select_fusion), channel_id=1, source_target_pairs={{0,96},{1,97},{2,98},{3,99},{4,100},{5,101},{6,102},{7,103},{8,104... | collective-permute-start | bytes 6291464 | tf_op jit(solution)/shard_map/ppermute | solution.py:28
  77.1 2.4 fusion.82
  79.4 86.7 %collective-permute-done.3 = f32[16,128,256]{2,0,1:T(8,128)S(1)} collective-permute-done((f32[16,128,256]{2,0,1:T(8,128)S(1)}, f32[16,128,256]{2,0,1:T(8,128)S(1)}, u32[]{:S(2)}, u32[]{:S(2)}) %collective-permute-start.3) | collective-permute-done | bytes 2097184 | tf_op jit(solution)/shard_map/ppermute | solution.py:28
  166.4 3.5 collective-permute-start.4
  170.0 2.5 fusion.84
  172.5 74.7 %collective-permute-done.4 = f32[16,128,256]{2,0,1:T(8,128)S(1)} collective-permute-done((f32[16,128,256]{2,0,1:T(8,128)S(1)}, f32[16,128,256]{2,0,1:T(8,128)S(1)}, u32[]{:S(2)}, u32[]{:S(2)}) %collective-permute-start.4) | collective-permute-done | bytes 2097184 | tf_op jit(solution)/shard_map/ppermute | solution.py:28
  247.4 2.5 copy.35
  250.0 1.7 reshape.1215
  251.7 1.1 fusion.73
  252.9 0.7 fusion.79
  253.5 0.7 fusion.81
  254.4 1.2 fusion.11
  255.5 0.6 copy.60
  256.2 0.7 copy-done.2
  256.8 1.0 slice_multiply_fusion
  257.8 1.2 mul.479
  259.0 4.1 multiply_add_fusion
  263.2 2.4 fusion.86
  265.6 2.5 fusion.88
  268.1 0.7 fusion.75
  268.8 0.7 fusion.77
  269.6 81.0 %collective-permute-start.5 = (f32[1,4,32768]{2,1,0:T(4,128)}, f32[1,4,32768]{2,1,0:T(4,128)}, u32[]{:S(2)}, u32[]{:S(2)}) collective-permute-start(f32[1,4,32768]{2,1,0:T(4,128)} %get-tuple-element.41), channel_id=1, source_target_pairs={{0,1},{1,2},{2,3},{3,4},{4,5},{5,6},{6,7},{7,8},{8,9},{9,10},{10,1... | collective-permute-start | bytes 1572872 | tf_op jit(solution)/shard_map/ppermute | solution.py:17
  350.6 1.2 fusion.14
  351.8 0.6 copy.57
  352.4 1.3 slice.426
  353.7 2.4 reshape.1221
  356.3 0.8 collective-permute-done.5
  357.1 4.6 %collective-permute-done.6 = f32[1,4,32768]{2,1,0:T(4,128)} collective-permute-done((f32[1,4,32768]{2,1,0:T(4,128)}, f32[1,4,32768]{2,1,0:T(4,128)}, u32[]{:S(2)}, u32[]{:S(2)}) %collective-permute-start.6) | collective-permute-done | bytes 524320 | tf_op jit(solution)/shard_map/ppermute | solution.py:19
  361.6 1.6 pad_maximum_fusion
  363.3 2.5 fusion.2
  365.8 2.2 fusion.62
  368.0 2.7 fusion.64
  370.7 2.7 fusion.66
  374.2 1.1 slice_multiply_fusion.1
  375.3 1.2 mul.476
  376.4 3.1 fusion.35
  379.5 4.0 fusion.8
  384.5 1.2 copy-done.16
  386.4 1.3 slice.384
  387.7 1.2 reshape.1220
  388.9 2.4 reshape.1219
  391.3 3.1 pad_maximum_fusion.3
  394.6 8.4 %fusion.28 = (f32[16,16384]{1,0:T(8,128)}, f32[1,16,16384]{2,1,0:T(8,128)S(1)}, f32[16,16384]{1,0:T(8,128)S(1)}, f32[16,16384]{1,0:T(8,128)S(1)}) fusion(f32[2,8,128,128]{3,2,1,0:T(8,128)S(1)} %bitcast.125, f32[2,8,128,128]{3,2,1,0:T(8,128)S(1)} %bitcast.127, f32[2,8,128,128]{3,2,1,0:T(8,128)S(1)} %bitcast.129, f32[]{:T(128)S(6)} %mul.452, f32[]{:T(128)} %bitcast.6, ...), kind=kLoop, calls=%fused_computation.50 | loop fusion | flops 9961472 | bytes 19925636 | tf_op jit(solution)/shard_map/mul | solution.py:74
  403.1 2.8 subtract_multiply_fusion
  406.0 1.2 add_multiply_fusion
  407.2 1.5 pad_maximum_fusion.2
  408.7 3.9 fusion.23
  (93 shorter events, 6.0 us)
Async XLA Ops:
  8.1 1.9 copy-start.18
  10.0 1.0 copy-start.14
  10.3 2.8 copy-start.10
  10.3 2.8 copy-start.12
  10.9 2.2 copy-start.4
  13.1 51.0 %collective-permute-start.2 = (f32[16,128,256]{2,0,1:T(8,128)}, f32[16,128,256]{2,0,1:T(8,128)}, u32[]{:S(2)}, u32[]{:S(2)}) collective-permute-start(f32[16,128,256]{2,0,1:T(8,128)} %pad_maximum_fusion.1), channel_id=1, source_target_pairs={{0,112},{1,113},{2,114},{3,115},{4,116},{5,117},{6,118},{7,119},{8... | collective-permute-start | bytes 6291464 | tf_op jit(solution)/shard_map/ppermute | solution.py:28
  14.1 8.4 %collective-permute-start = (f32[1,4,16384]{2,1,0:T(4,128)}, f32[1,4,16384]{2,1,0:T(4,128)S(1)}, u32[]{:S(2)}, u32[]{:S(2)}) collective-permute-start(f32[1,4,16384]{2,1,0:T(4,128)} %get-tuple-element.37), channel_id=1, source_target_pairs={{0,1},{1,2},{2,3},{3,4},{4,5},{5,6},{6,7},{7,8},{8,9},{9,10},{10,1... | collective-permute-start | bytes 786440 | tf_op jit(solution)/shard_map/ppermute | solution.py:17
  15.9 8.3 %collective-permute-start.1 = (f32[1,4,16384]{2,1,0:T(4,128)}, f32[1,4,16384]{2,1,0:T(4,128)}, u32[]{:S(2)}, u32[]{:S(2)}) collective-permute-start(f32[1,4,16384]{2,1,0:T(4,128)} %get-tuple-element.38), channel_id=1, source_target_pairs={{1,0},{2,1},{3,2},{4,3},{5,4},{6,5},{7,6},{8,7},{9,8},{10,9},{11,1... | collective-permute-start | bytes 786440 | tf_op jit(solution)/shard_map/ppermute | solution.py:19
  17.6 1.7 copy-start.30
  17.6 1.8 copy-start.29
  25.4 38.8 %copy-start.11 = (f32[16,128,128]{2,0,1:T(8,128)S(1)}, f32[16,128,128]{2,0,1:T(8,128)}, u32[]{:S(2)}) copy-start(f32[16,128,128]{2,0,1:T(8,128)} %copy-done.10) | copy-start | bytes 3145732
  25.4 38.8 %copy-start.13 = (f32[16,128,128]{2,0,1:T(8,128)S(1)}, f32[16,128,128]{2,0,1:T(8,128)}, u32[]{:S(2)}) copy-start(f32[16,128,128]{2,0,1:T(8,128)} %copy-done.12) | copy-start | bytes 3145732
  25.4 38.8 %copy-start.15 = (f32[16,128,64]{2,0,1:T(8,128)S(1)}, f32[16,128,64]{2,0,1:T(8,128)}, u32[]{:S(2)}) copy-start(f32[16,128,64]{2,0,1:T(8,128)} %copy-done.14) | copy-start | bytes 1572868
  27.2 142.8 %copy-start = (f32[1,20,16384]{2,1,0:T(8,128)}, f32[1,20,16384]{2,1,0:T(8,128)S(1)}, u32[]{:S(2)}) copy-start(f32[1,20,16384]{2,1,0:T(8,128)S(1)} %fusion.17) | copy-start | bytes 3932164
  66.8 99.4 %collective-permute-start.3 = (f32[16,128,256]{2,0,1:T(8,128)S(1)}, f32[16,128,256]{2,0,1:T(8,128)S(1)}, u32[]{:S(2)}, u32[]{:S(2)}) collective-permute-start(f32[16,128,256]{2,0,1:T(8,128)S(1)} %broadcast_select_fusion), channel_id=1, source_target_pairs={{0,96},{1,97},{2,98},{3,99},{4,100},{5,101},{6,102},{7,103},{8,104... | collective-permute-start | bytes 6291464 | tf_op jit(solution)/shard_map/ppermute | solution.py:28
  166.4 80.7 %collective-permute-start.4 = (f32[16,128,256]{2,0,1:T(8,128)S(1)}, f32[16,128,256]{2,0,1:T(8,128)S(1)}, u32[]{:S(2)}, u32[]{:S(2)}) collective-permute-start(f32[16,128,256]{2,0,1:T(8,128)S(1)} %broadcast_select_fusion.1), channel_id=1, source_target_pairs={{0,64},{1,65},{2,66},{3,67},{4,68},{5,69},{6,70},{7,71},{8,72},{9,... | collective-permute-start | bytes 6291464 | tf_op jit(solution)/shard_map/ppermute | solution.py:28
  255.5 1.3 copy-start.2
  265.6 2.5 copy-start.3
  269.6 87.4 %collective-permute-start.5 = (f32[1,4,32768]{2,1,0:T(4,128)}, f32[1,4,32768]{2,1,0:T(4,128)}, u32[]{:S(2)}, u32[]{:S(2)}) collective-permute-start(f32[1,4,32768]{2,1,0:T(4,128)} %get-tuple-element.41), channel_id=1, source_target_pairs={{0,1},{1,2},{2,3},{3,4},{4,5},{5,6},{6,7},{7,8},{8,9},{9,10},{10,1... | collective-permute-start | bytes 1572872 | tf_op jit(solution)/shard_map/ppermute | solution.py:17
  350.6 11.0 %collective-permute-start.6 = (f32[1,4,32768]{2,1,0:T(4,128)}, f32[1,4,32768]{2,1,0:T(4,128)}, u32[]{:S(2)}, u32[]{:S(2)}) collective-permute-start(f32[1,4,32768]{2,1,0:T(4,128)} %get-tuple-element.42), channel_id=1, source_target_pairs={{1,0},{2,1},{3,2},{4,3},{5,4},{6,5},{7,6},{8,7},{9,8},{10,9},{11,1... | collective-permute-start | bytes 1572872 | tf_op jit(solution)/shard_map/ppermute | solution.py:19
  374.2 2.3 copy-start.1
  376.4 3.1 copy-start.17
  384.2 1.6 copy-start.16
  391.3 3.2 copy-start.5
  391.3 3.2 copy-start.6
  391.3 3.2 copy-start.23
  391.3 3.2 copy-start.24
  394.5 8.5 %copy-start.7 = (f32[1,16,16384]{2,1,0:T(8,128)S(1)}, f32[1,16,16384]{2,1,0:T(8,128)}, u32[]{:S(2)}) copy-start(f32[1,16,16384]{2,1,0:T(8,128)} %reshape.1221) | copy-start | bytes 3145732
  394.5 8.5 %copy-start.8 = (f32[1,16,16384]{2,1,0:T(8,128)S(1)}, f32[1,16,16384]{2,1,0:T(8,128)}, u32[]{:S(2)}) copy-start(f32[1,16,16384]{2,1,0:T(8,128)} %reshape.1220) | copy-start | bytes 3145732
  394.5 8.5 %copy-start.9 = (f32[1,16,16384]{2,1,0:T(8,128)S(1)}, f32[1,16,16384]{2,1,0:T(8,128)}, u32[]{:S(2)}) copy-start(f32[1,16,16384]{2,1,0:T(8,128)} %reshape.1219) | copy-start | bytes 3145732
  394.5 8.5 %copy-start.19 = (f32[1,16,16383]{2,1,0:T(8,128)S(1)}, f32[1,16,16383]{2,1,0:T(8,128)}, u32[]{:S(2)}) copy-start(f32[1,16,16383]{2,1,0:T(8,128)} %get-tuple-element.59) | copy-start | bytes 3145540
  394.5 8.5 %copy-start.20 = (f32[1,16,16383]{2,1,0:T(8,128)S(1)}, f32[1,16,16383]{2,1,0:T(8,128)}, u32[]{:S(2)}) copy-start(f32[1,16,16383]{2,1,0:T(8,128)} %get-tuple-element.62) | copy-start | bytes 3145540
  394.5 8.5 %copy-start.21 = (f32[1,16,16382]{2,1,0:T(8,128)S(1)}, f32[1,16,16382]{2,1,0:T(8,128)}, u32[]{:S(2)}) copy-start(f32[1,16,16382]{2,1,0:T(8,128)} %get-tuple-element.67) | copy-start | bytes 3145348
  394.6 8.5 %copy-start.22 = (f32[1,16,16382]{2,1,0:T(8,128)S(1)}, f32[1,16,16382]{2,1,0:T(8,128)}, u32[]{:S(2)}) copy-start(f32[1,16,16382]{2,1,0:T(8,128)} %get-tuple-element.70) | copy-start | bytes 3145348
  394.6 8.5 %copy-start.25 = (f32[1,16,16383]{2,1,0:T(8,128)S(1)}, f32[1,16,16383]{2,1,0:T(8,128)}, u32[]{:S(2)}) copy-start(f32[1,16,16383]{2,1,0:T(8,128)} %get-tuple-element.75) | copy-start | bytes 3145540
  394.6 8.5 %copy-start.26 = (f32[1,16,16383]{2,1,0:T(8,128)S(1)}, f32[1,16,16383]{2,1,0:T(8,128)}, u32[]{:S(2)}) copy-start(f32[1,16,16383]{2,1,0:T(8,128)} %get-tuple-element.78) | copy-start | bytes 3145540
  394.6 8.5 %copy-start.27 = (f32[1,16,16382]{2,1,0:T(8,128)S(1)}, f32[1,16,16382]{2,1,0:T(8,128)}, u32[]{:S(2)}) copy-start(f32[1,16,16382]{2,1,0:T(8,128)} %get-tuple-element.83) | copy-start | bytes 3145348
  394.6 8.5 %copy-start.28 = (f32[1,16,16382]{2,1,0:T(8,128)S(1)}, f32[1,16,16382]{2,1,0:T(8,128)}, u32[]{:S(2)}) copy-start(f32[1,16,16382]{2,1,0:T(8,128)} %get-tuple-element.86) | copy-start | bytes 3145348
where the time goes:
time: 421 us; the launch traced here: 413 us
  waiting for transfers between devices  205 us (49%)
  starting transfers between devices  96.7 us (23%)
  other arithmetic  53.8 us (13%)
  local copies, waits for them, and re-layouts  53.1 us (13%)
    ppermute x3, waiting for transfers between devices, passed_along(): return lax.ppermute(x, axis, [(i, (i + by) % size) for i in range(size)])  198 us
    ppermute x2, starting transfers between devices, with_halo(): lax.ppermute(tail, axis, [(i, (i + 1) % count) for i in range(count)])  82.8 us
    ppermute x3, starting transfers between devices, passed_along(): return lax.ppermute(x, axis, [(i, (i + by) % size) for i in range(size)])  13.8 us
  transfers between devices with their start and end apart: 7, of which 6 were waited for; matrix products, arithmetic and copies ran while one was open for 4% of the time, Pallas kernels for 0%

commit v1 on v0

v1 whole, which is shorter than its diff:
```python
import functools

import jax
import jax.numpy as jnp
from jax import lax
from jax.experimental import pallas as pl
from jax.experimental.pallas import tpu as pltpu
from jax.sharding import PartitionSpec as P

RB = 8
LANES = 128
EDGE = 8
STRIDE = 32
CAPS = (16, 18, 20, 22, 24, 28, 32, 48, 128)
C1, C2 = 8.0 / 12.0, 1.0 / 12.0
VMEM = pl.BlockSpec(memory_space=pltpu.VMEM)
SMEM = pl.BlockSpec(memory_space=pltpu.SMEM)


def lanes_of(rows):
    return lax.broadcasted_iota(jnp.int32, (rows, LANES), 1)


def params(mib):
    return pltpu.CompilerParams(vmem_limit_bytes=mib * 2**20)


def tiles_of(cap):
    return 2 * cap + -(-cap // 8)


def first(ahead, behind, ahead2, behind2):
    return C1 * (ahead - behind) - C2 * (ahead2 - behind2)


def second(centre, pairs):
    one, two, three, four = pairs
    return (four - 16.0 * three + 64.0 * two + 16.0 * one - 130.0 * centre) * (1.0 / 144.0)


def rows_of(window):
    def at(k):
        return window[8 + k : 24 + k, :]

    a1, b1, a2, b2 = at(1), at(-1), at(2), at(-2)
    slope = first(a1, b1, a2, b2)
    curve = second(at(0), (a1 + b1, a2 + b2, at(3) + at(-3), at(4) + at(-4)))
    return slope, curve


def slope_rows(window):
    def at(k):
        return window[8 + k : 24 + k, :]

    return first(at(1), at(-1), at(2), at(-2))


def shifted(field, beside, k, lane):
    if k > 0:
        return pltpu.roll(jnp.where(lane < k, beside, field), LANES - k, 1)
    return pltpu.roll(jnp.where(lane >= LANES + k, beside, field), -k, 1)


def columns_of(field, beside, slope, slope_beside, lane):
    def at(k):
        return shifted(field, beside, k, lane)

    a1, b1, a2, b2 = at(1), at(-1), at(2), at(-2)
    slope_c = first(a1, b1, a2, b2)
    curve_cc = second(field, (a1 + b1, a2 + b2, at(3) + at(-3), at(4) + at(-4)))

    def of_slope(k):
        return shifted(slope, slope_beside, k, lane)

    curve_rc = first(of_slope(1), of_slope(-1), of_slope(2), of_slope(-2))
    return slope_c, curve_rc, curve_cc


def near_kernel(blocks, p_ref, up_ref, down_ref, r_ref, c_ref, rr_ref, rc_ref, cc_ref, f_ref):
    lane = lanes_of(16)

    def rows(b, _):
        col = pl.multiple_of(b * LANES, LANES)
        base = pl.multiple_of(b * STRIDE, STRIDE)
        out = pl.multiple_of(b * 16, 16)
        window = f_ref.at[pl.ds(base, STRIDE), :]
        window[4:8, :] = up_ref[:, pl.ds(col, LANES)]
        window[8:24, :] = p_ref[:, pl.ds(col, LANES)]
        window[24:28, :] = down_ref[:, pl.ds(col, LANES)]
        slope, curve = rows_of(window)
        r_ref[pl.ds(out, 16), :] = slope
        rr_ref[pl.ds(out, 16), :] = curve
        return 0

    lax.fori_loop(0, blocks, rows, 0, unroll=4)

    def columns(b, _):
        before = lax.rem(b + (blocks - 1), blocks)
        after = lax.rem(b + 1, blocks)

        def of(i):
            return p_ref[:, pl.ds(pl.multiple_of(i * LANES, LANES), LANES)]

        def slope_of(i):
            return r_ref[pl.ds(pl.multiple_of(i * 16, 16), 16), :]

        far = lane >= LANES // 2
        slope_c, curve_rc, curve_cc = columns_of(
            of(b),
            jnp.where(far, of(before), of(after)),
            slope_of(b),
            jnp.where(far, slope_of(before), slope_of(after)),
            lane,
        )
        out = pl.ds(pl.multiple_of(b * 16, 16), 16)
        c_ref[out, :] = slope_c
        rc_ref[out, :] = curve_rc
        cc_ref[out, :] = curve_cc
        return 0

    lax.fori_loop(0, blocks, columns, 0, unroll=2)


def near_fields(potentials, up, down):
    height, width = potentials.shape[1:]
    blocks = width // LANES
    shape = jax.ShapeDtypeStruct((blocks * 16, LANES), jnp.float32)
    return pl.pallas_call(
        functools.partial(near_kernel, blocks),
        grid=(1,),
        out_shape=(shape,) * 5,
        in_specs=[pl.BlockSpec((None, height, width), lambda i: (0, 0, 0)), VMEM, VMEM],
        out_specs=(VMEM,) * 5,
        scratch_shapes=[pltpu.VMEM((blocks * STRIDE, LANES), jnp.float32)],
        compiler_params=params(16),
        cost_estimate=pl.CostEstimate(flops=60_000_000, bytes_accessed=7_000_000, transcendentals=0),
        name="near_fields",
    )(potentials, up, down)


def pack_kernel(blocks, cap, where_ref, shift_ref, slot_ref, source_ref, p_ref, out_ref):
    here = where_ref[0]
    tall = tiles_of(cap) * 8
    lane = lanes_of(8)
    far = lane >= LANES // 2

    def block(b, _):
        slot = slot_ref[b]
        source = source_ref[b]
        start = lax.rem(here + RB - shift_ref[b], RB) * tall
        before = lax.rem(source + (blocks - 1), blocks)
        after = lax.rem(source + 1, blocks)

        def of(i):
            return p_ref[:, pl.ds(pl.multiple_of(i * LANES, LANES), LANES)]

        out_ref[pl.ds(pl.multiple_of(start + slot * 16, 8), 16), :] = of(source)
        left, right = of(before), of(after)
        place = lax.rem(slot, 8) * EDGE
        row = pl.ds(pl.multiple_of(start + 16 * cap + lax.div(slot, 8) * 8, 8), 8)
        for half in range(2):
            top = 8 * half
            edge = jnp.where(far, left[top : top + 8], right[top : top + 8])
            spot = place + half * (LANES // 2)
            moved = pltpu.roll(edge, spot + EDGE // 2, 1)
            mask = (lane >= spot) & (lane < spot + EDGE)
            pltpu.store(out_ref.at[row, :], moved, mask=mask)
        return 0

    lax.fori_loop(0, blocks, block, 0, unroll=4)


def pack(cap, where, shift, slot, source, potentials):
    height, width = potentials.shape[1:]
    blocks = width // LANES
    return pl.pallas_call(
        functools.partial(pack_kernel, blocks, cap),
        grid=(1,),
        out_shape=jax.ShapeDtypeStruct((RB * tiles_of(cap) * 8, LANES), jnp.float32),
        in_specs=[SMEM] * 4 + [pl.BlockSpec((None, height, width), lambda i: (1, 0, 0))],
        out_specs=VMEM,
        compiler_params=params(16),
        cost_estimate=pl.CostEstimate(flops=2_000_000, bytes_accessed=3_000_000, transcendentals=0),
        name="pack_blocks",
    )(where, shift, slot, source, potentials)


def unpack_kernel(blocks, cap, where_ref, shift_ref, slot_ref, in_ref, w_ref, h_ref, head_ref, tail_ref):
    here = where_ref[0]
    tall = tiles_of(cap) * 8
    lane = lanes_of(8)

    def block(b, _):
        slot = slot_ref[b]
        start = lax.rem(here + shift_ref[b], RB) * tall
        tile = in_ref[pl.ds(pl.multiple_of(start + slot * 16, 8), 16), :]
        col = pl.ds(pl.multiple_of(b * LANES, LANES), LANES)
        w_ref[pl.ds(pl.multiple_of(b * 16, 16), 16), :] = tile
        head_ref[:, col] = tile[0:4]
        tail_ref[:, col] = tile[12:16]
        edge = in_ref[pl.ds(pl.multiple_of(start + 16 * cap + lax.div(slot, 8) * 8, 8), 8), :]
        place = lax.rem(slot, 8) * EDGE
        spot = lax.rem(b, 16) * EDGE
        mask = (lane >= spot) & (lane < spot + EDGE)
        for half in range(2):
            turn = lax.rem(spot + 2 * LANES - place - half * (LANES // 2), LANES)
            row = pl.ds(pl.multiple_of(lax.div(b, 16) * 16 + 8 * half, 8), 8)
            pltpu.store(h_ref.at[row, :], pltpu.roll(edge, turn, 1), mask=mask)
        return 0

    lax.fori_loop(0, blocks, block, 0, unroll=4)
    for g in range(blocks // 16):
        col = slice((blocks + g) * LANES, (blocks + g + 1) * LANES)
        head_ref[:, col] = h_ref[16 * g : 16 * g + 4, :]
        tail_ref[:, col] = h_ref[16 * g + 12 : 16 * g + 16, :]


def unpack(cap, blocks, where, shift, slot, arrived):
    ends = jax.ShapeDtypeStruct((4, (blocks + blocks // 16) * LANES), jnp.float32)
    return pl.pallas_call(
        functools.partial(unpack_kernel, blocks, cap),
        out_shape=(
            jax.ShapeDtypeStruct((blocks * 16, LANES), jnp.float32),
            jax.ShapeDtypeStruct((blocks, LANES), jnp.float32),
            ends,
            ends,
        ),
        in_specs=[SMEM] * 3 + [VMEM],
        out_specs=(VMEM,) * 4,
        compiler_params=params(16),
        cost_estimate=pl.CostEstimate(flops=2_000_000, bytes_accessed=3_000_000, transcendentals=0),
        name="unpack_blocks",
    )(where, shift, slot, arrived)


def far_kernel(
    ratio_ref, w_ref, h_ref, up_ref, down_ref, uph_ref, downh_ref, r_ref, c_ref, rr_ref, rc_ref, cc_ref,
    conv_ref, shear_ref, rot_ref, disp_ref, f_ref, e_ref, s_ref,
):
    lane = lanes_of(16)
    near_to_two, near_to_source, two_to_source = ratio_ref[0], ratio_ref[1], ratio_ref[2]
    half_one, half_two = 0.5 * near_to_source, 0.5 * two_to_source
    e_ref[4:8, :] = uph_ref[...]
    e_ref[8:24, :] = h_ref[...]
    e_ref[24:28, :] = downh_ref[...]
    s_ref[...] = slope_rows(e_ref)

    def block(b, _):
        col = pl.ds(pl.multiple_of(b * LANES, LANES), LANES)
        tile = pl.ds(pl.multiple_of(b * 16, 16), 16)
        window = f_ref.at[pl.ds(pl.multiple_of(b * STRIDE, STRIDE), STRIDE), :]
        centre = w_ref[tile, :]
        window[4:8, :] = up_ref[:, col]
        window[8:24, :] = centre
        window[24:28, :] = down_ref[:, col]
        far_r, far_rr = rows_of(window)
        turn = LANES - EDGE // 2 - b * EDGE
        beside = pltpu.roll(e_ref[8:24, :], turn, 1)
        slope_beside = pltpu.roll(s_ref[...], turn, 1)
        far_c, far_rc, far_cc = columns_of(centre, beside, far_r, slope_beside, lane)
        near_rr, near_rc, near_cc = rr_ref[tile, :], rc_ref[tile, :], cc_ref[tile, :]
        inner_rr = 1.0 - near_to_two * near_rr
        inner_rc = -near_to_two * near_rc
        inner_cc = 1.0 - near_to_two * near_cc
        chain_rr = far_rr * inner_rr + far_rc * inner_rc
        chain_rc = far_rr * inner_rc + far_rc * inner_cc
        chain_cr = far_rc * inner_rr + far_cc * inner_rc
        chain_cc = far_rc * inner_rc + far_cc * inner_cc
        conv_ref[:, col] = half_one * (near_rr + near_cc) + half_two * (chain_rr + chain_cc)
        shear_ref[0, :, col] = half_one * (near_cc - near_rr) + half_two * (chain_cc - chain_rr)
        shear_ref[1, :, col] = near_to_source * near_rc + half_two * (chain_rc + chain_cr)
        rot_ref[:, col] = half_two * (chain_cr - chain_rc)
        disp_ref[0, :, col] = near_to_source * r_ref[tile, :] + two_to_source * far_r
        disp_ref[1, :, col] = near_to_source * c_ref[tile, :] + two_to_source * far_c
        return 0

    lax.fori_loop(0, 16, block, 0, unroll=2)


def assemble(ratios, windows, edges, above, below, near):
    blocks = windows.shape[0] // 16
    steps = blocks // 16
    wide = 16 * LANES
    field = pl.BlockSpec((256, LANES), lambda i: (i, 0))
    ends = pl.BlockSpec((4, wide), lambda i: (0, i))
    edge_ends = pl.BlockSpec((4, LANES), lambda i: (0, blocks + i))
    flat = jax.ShapeDtypeStruct((16, blocks * LANES), jnp.float32)
    pair = jax.ShapeDtypeStruct((2, 16, blocks * LANES), jnp.float32)
    flat_spec = pl.BlockSpec((16, wide), lambda i: (0, i))
    pair_spec = pl.BlockSpec((2, 16, wide), lambda i: (0, 0, i))
    return pl.pallas_call(
        far_kernel,
        grid=(steps,),
        out_shape=(flat, pair, flat, pair),
        in_specs=[SMEM, field, pl.BlockSpec((16, LANES), lambda i: (i, 0)), ends, ends, edge_ends, edge_ends]
        + [field] * 5,
        out_specs=(flat_spec, pair_spec, flat_spec, pair_spec),
        scratch_shapes=[
            pltpu.VMEM((16 * STRIDE, LANES), jnp.float32),
            pltpu.VMEM((STRIDE, LANES), jnp.float32),
            pltpu.VMEM((16, LANES), jnp.float32),
        ],
        compiler_params=params(16),
        name="far_fields",
    )(ratios, windows, edges, above, below, above, below, *near)


def passed(x, by):
    size = lax.axis_size("row")
    return lax.ppermute(x, "row", [(i, (i + by) % size) for i in range(size)])


def per_device(potentials, ratios, row_offset, col_offset):
    devices = lax.axis_size("row")
    stride = devices // RB
    height, width = potentials.shape[1:]
    blocks = width // LANES
    index = jnp.arange(blocks, dtype=jnp.int32)
    source = (index + col_offset) % blocks
    alike = (row_offset[:, None] == row_offset[None, :]) & (index[None, :] < index[:, None])
    slot = jnp.sum(alike.astype(jnp.int32), axis=1)
    needed = jnp.max(slot) + 1
    where = (lax.axis_index("row") // stride).astype(jnp.int32).reshape(1)
    groups = [[level * stride + j for level in range(RB)] for j in range(stride)]
    above1 = passed(potentials[0, height - 4 :, :], 1)
    below1 = passed(potentials[0, :4, :], -1)
    caps = tuple(c for c in CAPS if c < blocks) + (blocks,)

    def exchange(cap, potentials, above1, below1, where, shift, slot, source):
        packed = pack(cap, where, shift, slot, source, potentials)
        packed = packed.reshape(RB, tiles_of(cap) * 8, LANES)
        arrived = lax.all_to_all(packed, "row", 0, 0, axis_index_groups=groups)
        near = near_fields(potentials, above1, below1)
        arrived = arrived.reshape(RB * tiles_of(cap) * 8, LANES)
        return unpack(cap, blocks, where, shift, slot, arrived), near

    level = jnp.sum((needed > jnp.asarray(caps[:-1], jnp.int32)).astype(jnp.int32))
    (windows, edges, heads, tails), near = lax.switch(
        level,
        [functools.partial(exchange, cap) for cap in caps],
        potentials, above1, below1, where, row_offset, slot, source,
    )
    above = passed(tails, 1)
    below = passed(heads, -1)
    return assemble(ratios, windows, edges, above, below, near)


def solution(mesh):
    return jax.shard_map(
        per_device,
        mesh=mesh,
        in_specs=(P("cosmo", "row", None), P("cosmo"), P("cosmo"), P("cosmo")),
        out_specs=(
            P(("cosmo", "row"), None),
            P(None, ("cosmo", "row"), None),
            P(("cosmo", "row"), None),
            P(None, ("cosmo", "row"), None),
        ),
        check_vma=False,
    )
```

time: 421 us -> 104 us (0.25)
  the two profiles are of different devices: /device:TPU:543 before, /device:TPU:527 now
where the time goes in v1:
time: 104 us
  Pallas kernels  38.5 us (37%)
  waiting for transfers between devices  31.6 us (30%)
  starting transfers between devices  26.9 us (26%)
  other arithmetic  3.5 us (3%)
  between operations  1.95 us (2%)
  local copies, waits for them, and re-layouts  1.31 us (1%)
    all_to_all x1, starting transfers between devices, exchange(): arrived = lax.all_to_all(packed, 'row', 0, 0, axis_index_groups=groups)  21.8 us
    all_to_all x1, waiting for transfers between devices, exchange(): arrived = lax.all_to_all(packed, 'row', 0, 0, axis_index_groups=groups)  20.1 us
    pallas_call x1, Pallas kernels, assemble(): pl.pallas_call(far_kernel, grid=(steps,), out_shape=(flat, pair, flat, pa...  15.4 us
    pallas_call x1, Pallas kernels, near_fields(): pl.pallas_call(functools.partial(near_kernel, blocks), grid=(1,), out_sha...  12.6 us
    ppermute x4, waiting for transfers between devices, passed(): return lax.ppermute(x, 'row', [(i, (i + by) % size) for i in range(size)])  11.5 us
    pallas_call x1, Pallas kernels, pack(): pl.pallas_call(functools.partial(pack_kernel, blocks, cap), grid=(1,), ou...  5.5 us
    ppermute x4, starting transfers between devices, passed(): return lax.ppermute(x, 'row', [(i, (i + by) % size) for i in range(size)])  5.1 us
    pallas_call x1, Pallas kernels, unpack(): pl.pallas_call(functools.partial(unpack_kernel, blocks, cap), out_shape=(...  4.93 us
  transfers between devices with their start and end apart: 5, of which 4 were waited for; matrix products, arithmetic and copies ran while one was open for 3% of the time, Pallas kernels for 12%

profile of v1, /device:TPU:527, one launch (start us, length us, event | category | flops | bytes accessed | tf_op | source)
XLA Modules:
  0.0 103.8 jit_solution(6696832203440573579)
XLA Ops:
  0.6 1.3 %slice_bitcast_fusion = (f32[4,16384]{1,0:T(4,128)S(1)}, f32[4,16384]{1,0:T(4,128)S(1)}) fusion(f32[2,16,16384]{2,1,0:T(8,128)} %param.14), kind=kLoop, calls=%fused_computation | loop fusion | bytes 1048576 | tf_op jit(solution)/shard_map/squeeze | solution.py:326
  1.9 2.0 %collective-permute-start = (f32[4,16384]{1,0:T(4,128)S(1)}, f32[4,16384]{1,0:T(4,128)}, u32[]{:S(2)}, u32[]{:S(2)}) collective-permute-start(f32[4,16384]{1,0:T(4,128)S(1)} %get-tuple-element.293), channel_id=1, source_target_pairs={{0,1},{1,2},{2,3},{3,4},{4,5},{5,6},{6,7},{7,8},{8,9},{9,10},{10,1... | collective-permute-start | bytes 786440 | tf_op jit(solution)/shard_map/ppermute | solution.py:310
  3.9 0.0 collective-permute-start.1
  3.9 0.9 convert_reduce_fusion
  4.8 0.6 reduce_max.9
  6.1 1.3 %fusion.1 = s32[]{:T(128)} fusion(s32[8]{0:T(128)} %constant.42.clone, s32[]{:T(128)S(6)} %add.13), kind=kLoop, calls=%fused_computation.9 | loop fusion | flops 23 | bytes 40 | tf_op jit(solution)/shard_map/reduce_sum | solution.py:337
  8.0 0.7 and_select_fusion
  8.7 0.0 collective-permute-done
  8.7 3.2 %collective-permute-done.1 = f32[4,16384]{1,0:T(4,128)} collective-permute-done((f32[4,16384]{1,0:T(4,128)S(1)}, f32[4,16384]{1,0:T(4,128)}, u32[]{:S(2)}, u32[]{:S(2)}) %collective-permute-start.1) | collective-permute-done | bytes 262176 | tf_op jit(solution)/shard_map/ppermute | solution.py:310
  11.9 0.0 copy-start.3
  11.9 65.0 %conditional.1 = (f32[2048,128]{1,0:T(8,128)}, f32[128,128]{1,0:T(8,128)}, f32[4,17408]{1,0:T(4,128)}, f32[4,17408]{1,0:T(4,128)}, f32[2048,128]{1,0:T(8,128)}, ...) conditional(s32[]{:T(128)} %clamp.3, (s32[1]{0:T(128)}, ...), branch_computations={%region_3.4_spmd, %region_4.5_spmd, %region_5.6_spmd, %region_6.7_... | conditional | flops 64000000 | bytes 85878336 | solution.py:338
  11.9 5.5 %pack_blocks.12 = f32[3008,128]{1,0:T(8,128)} custom-call(s32[1]{0:T(128)} %get-tuple-element.174.where_ref, s32[128]{0:T(128)} %get-tuple-element.175.shift_ref, s32[128]{0:T(128)S(1)} %get-tuple-element.176.slot_ref, s32[128]{0:T(128)S(1)} %get-tuple-element.177.source_ref, f32[2,16,16384]{2,1,0:T(8,128)} %get-tuple-element.178.p_ref), custom_call_target="tpu_custom_call" | custom-call | flops 2000000 | bytes 3000000 | tf_op jit(solution)/shard_map/cond/branch_3_fun/pack_blocks/pallas_call | solution.py:176
  17.4 0.0 copy-start.8
  17.4 0.0 copy-start.13
  17.4 21.8 %all-to-all-start.3 = ((f32[8,376,128]{2,1,0:T(8,128)}), f32[8,376,128]{2,1,0:T(8,128)S(1)}, u32[]{:S(2)}, u32[]{:S(2)}) async-start(f32[8,376,128]{2,1,0:T(8,128)} %bitcast.6), calls=%async_computation.3 | async-start | bytes 3080192 | tf_op jit(solution)/shard_map/cond/branch_3_fun/all_to_all | solution.py:332
  39.2 0.0 copy-start.21
  39.2 0.0 copy-done.8
  39.2 0.0 copy-done.13
  39.2 12.6 %near_fields.12 = (f32[2048,128]{1,0:T(8,128)}, f32[2048,128]{1,0:T(8,128)}, f32[2048,128]{1,0:T(8,128)}, f32[2048,128]{1,0:T(8,128)}, f32[2048,128]{1,0:T(8,128)}) custom-call(f32[2,16,16384]{2,1,0:T(8,128)} %get-tuple-element.178.p_ref, f32[4,16384]{1,0:T(4,128)S(1)} %copy-done.8, f32[4,16384]{1,0:T(4,128)S(1)} %copy-done.13), custom_call_target="tpu_custom_call" | custom-call | flops 60000000 | bytes 7000000 | tf_op jit(solution)/shard_map/cond/branch_3_fun/near_fields/pallas_call | solution.py:128
  51.9 20.1 %all-to-all-done.3 = f32[8,376,128]{2,1,0:T(8,128)S(1)} async-done(((f32[8,376,128]{2,1,0:T(8,128)}), f32[8,376,128]{2,1,0:T(8,128)S(1)}, u32[]{:S(2)}, u32[]{:S(2)}) %all-to-all-start.3) | async-done | bytes 1540128 | tf_op jit(solution)/shard_map/cond/branch_3_fun/all_to_all | solution.py:332
  72.0 0.0 copy-done.21
  72.0 4.9 %unpack_blocks.12 = (f32[2048,128]{1,0:T(8,128)}, f32[128,128]{1,0:T(8,128)}, f32[4,17408]{1,0:T(4,128)}, f32[4,17408]{1,0:T(4,128)}) custom-call(s32[1]{0:T(128)} %get-tuple-element.174.where_ref, s32[128]{0:T(128)S(1)} %copy-done.21, s32[128]{0:T(128)S(1)} %get-tuple-element.176.slot_ref, f32[3008,128]{1,0:T(8,128)S(1)} %bitcast.30), custom_call_target="tpu_custom_call" | custom-call | flops 2000000 | bytes 3000000 | tf_op jit(solution)/shard_map/cond/branch_3_fun/unpack_blocks/pallas_call | solution.py:220
  76.9 3.1 %collective-permute-start.2 = (f32[4,17408]{1,0:T(4,128)}, f32[4,17408]{1,0:T(4,128)S(1)}, u32[]{:S(2)}, u32[]{:S(2)}) collective-permute-start(f32[4,17408]{1,0:T(4,128)} %get-tuple-element.285), channel_id=1, source_target_pairs={{0,1},{1,2},{2,3},{3,4},{4,5},{5,6},{6,7},{7,8},{8,9},{9,10},{10,1... | collective-permute-start | bytes 835592 | tf_op jit(solution)/shard_map/ppermute | solution.py:310
  80.0 0.0 collective-permute-start.3
  80.1 3.8 %collective-permute-done.2.up_ref.uph_ref = f32[4,17408]{1,0:T(4,128)S(1)} collective-permute-done((f32[4,17408]{1,0:T(4,128)}, f32[4,17408]{1,0:T(4,128)S(1)}, u32[]{:S(2)}, u32[]{:S(2)}) %collective-permute-start.2) | collective-permute-done | bytes 278560 | tf_op jit(solution)/shard_map/ppermute | solution.py:310
  83.9 4.5 %collective-permute-done.3.down_ref.downh_ref = f32[4,17408]{1,0:T(4,128)S(1)} collective-permute-done((f32[4,17408]{1,0:T(4,128)}, f32[4,17408]{1,0:T(4,128)S(1)}, u32[]{:S(2)}, u32[]{:S(2)}) %collective-permute-start.3) | collective-permute-done | bytes 278560 | tf_op jit(solution)/shard_map/ppermute | solution.py:310
  88.3 0.0 copy-done.3
  88.3 15.4 %far_fields.1 = (f32[16,16384]{1,0:T(8,128)}, f32[2,16,16384]{2,1,0:T(8,128)}, f32[16,16384]{1,0:T(8,128)}, f32[2,16,16384]{2,1,0:T(8,128)}) custom-call(f32[3]{0:T(128)S(1)} %copy-done.3, f32[2048,128]{1,0:T(8,128)} %get-tuple-element.283.w_ref, f32[128,128]{1,0:T(8,128)} %get-tuple-element.284.h_ref, f32[4,17408]{1,0:T(4,128)S(1)} %collective-permute-done.2.up_ref.uph_ref, ...), custom_call_target="tpu_custom_call" | custom-call | tf_op jit(solution)/shard_map/far_fields/pallas_call | solution.py:291
Async XLA Ops:
  1.9 6.8 %collective-permute-start = (f32[4,16384]{1,0:T(4,128)S(1)}, f32[4,16384]{1,0:T(4,128)}, u32[]{:S(2)}, u32[]{:S(2)}) collective-permute-start(f32[4,16384]{1,0:T(4,128)S(1)} %get-tuple-element.293), channel_id=1, source_target_pairs={{0,1},{1,2},{2,3},{3,4},{4,5},{5,6},{6,7},{7,8},{8,9},{9,10},{10,1... | collective-permute-start | bytes 786440 | tf_op jit(solution)/shard_map/ppermute | solution.py:310
  3.9 8.0 %collective-permute-start.1 = (f32[4,16384]{1,0:T(4,128)S(1)}, f32[4,16384]{1,0:T(4,128)}, u32[]{:S(2)}, u32[]{:S(2)}) collective-permute-start(f32[4,16384]{1,0:T(4,128)S(1)} %get-tuple-element.292), channel_id=1, source_target_pairs={{0,127},{1,0},{2,1},{3,2},{4,3},{5,4},{6,5},{7,6},{8,7},{9,8},{10,... | collective-permute-start | bytes 786440 | tf_op jit(solution)/shard_map/ppermute | solution.py:310
  11.9 76.5 %copy-start.3 = (f32[3]{0:T(128)S(1)}, f32[3]{0:T(128)}, u32[]{:S(2)}) copy-start(f32[3]{0:T(128)} %ratio_ref.1) | copy-start | bytes 40
  17.4 21.8 %copy-start.8 = (f32[4,16384]{1,0:T(4,128)S(1)}, f32[4,16384]{1,0:T(4,128)}, u32[]{:S(2)}) copy-start(f32[4,16384]{1,0:T(4,128)} %get-tuple-element.183.up_ref) | copy-start | bytes 786436 | tf_op jit(solution)/shard_map/cond
  17.4 21.8 %copy-start.13 = (f32[4,16384]{1,0:T(4,128)S(1)}, f32[4,16384]{1,0:T(4,128)}, u32[]{:S(2)}) copy-start(f32[4,16384]{1,0:T(4,128)} %get-tuple-element.184.down_ref) | copy-start | bytes 786436 | tf_op jit(solution)/shard_map/cond
  17.4 54.6 %all-to-all-start.3 = ((f32[8,376,128]{2,1,0:T(8,128)}), f32[8,376,128]{2,1,0:T(8,128)S(1)}, u32[]{:S(2)}, u32[]{:S(2)}) async-start(f32[8,376,128]{2,1,0:T(8,128)} %bitcast.6), calls=%async_computation.3 | async-start | bytes 3080192 | tf_op jit(solution)/shard_map/cond/branch_3_fun/all_to_all | solution.py:332
  39.2 32.8 %copy-start.21 = (s32[128]{0:T(128)S(1)}, s32[128]{0:T(128)}, u32[]{:S(2)}) copy-start(s32[128]{0:T(128)} %get-tuple-element.175.shift_ref) | copy-start | bytes 1540 | tf_op jit(solution)/shard_map/cond
  76.9 7.0 %collective-permute-start.2 = (f32[4,17408]{1,0:T(4,128)}, f32[4,17408]{1,0:T(4,128)S(1)}, u32[]{:S(2)}, u32[]{:S(2)}) collective-permute-start(f32[4,17408]{1,0:T(4,128)} %get-tuple-element.285), channel_id=1, source_target_pairs={{0,1},{1,2},{2,3},{3,4},{4,5},{5,6},{6,7},{7,8},{8,9},{9,10},{10,1... | collective-permute-start | bytes 835592 | tf_op jit(solution)/shard_map/ppermute | solution.py:310
  80.0 8.3 %collective-permute-start.3 = (f32[4,17408]{1,0:T(4,128)}, f32[4,17408]{1,0:T(4,128)S(1)}, u32[]{:S(2)}, u32[]{:S(2)}) collective-permute-start(f32[4,17408]{1,0:T(4,128)} %get-tuple-element.286), channel_id=1, source_target_pairs={{0,127},{1,0},{2,1},{3,2},{4,3},{5,4},{6,5},{7,6},{8,7},{9,8},{10,... | collective-permute-start | bytes 835592 | tf_op jit(solution)/shard_map/ppermute | solution.py:310

commit v2 on v1

v2 whole, which is shorter than its diff:
```python
import functools

import jax
import jax.numpy as jnp
from jax import lax
from jax.experimental import pallas as pl
from jax.experimental.pallas import tpu as pltpu
from jax.sharding import PartitionSpec as P

RB = 8
LANES = 128
EDGE = 8
STRIDE = 32
CAPS = (18, 20, 21, 22, 23, 24, 26, 30)
C1, C2 = 8.0 / 12.0, 1.0 / 12.0
VMEM = pl.BlockSpec(memory_space=pltpu.VMEM)
SMEM = pl.BlockSpec(memory_space=pltpu.SMEM)


def lanes_of(rows):
    return lax.broadcasted_iota(jnp.int32, (rows, LANES), 1)


def params(mib):
    return pltpu.CompilerParams(vmem_limit_bytes=mib * 2**20)


def tiles_of(cap):
    return 2 * cap + -(-cap // 8)


def first(ahead, behind, ahead2, behind2):
    return C1 * (ahead - behind) - C2 * (ahead2 - behind2)


def second(centre, pairs):
    one, two, three, four = pairs
    return (four - 16.0 * three + 64.0 * two + 16.0 * one - 130.0 * centre) * (1.0 / 144.0)


def rows_of(window):
    def at(k):
        return window[8 + k : 24 + k, :]

    a1, b1, a2, b2 = at(1), at(-1), at(2), at(-2)
    slope = first(a1, b1, a2, b2)
    curve = second(at(0), (a1 + b1, a2 + b2, at(3) + at(-3), at(4) + at(-4)))
    return slope, curve


def slope_rows(window):
    def at(k):
        return window[8 + k : 24 + k, :]

    return first(at(1), at(-1), at(2), at(-2))


def shifted(field, beside, k, lane):
    if k > 0:
        return pltpu.roll(jnp.where(lane < k, beside, field), LANES - k, 1)
    return pltpu.roll(jnp.where(lane >= LANES + k, beside, field), -k, 1)


def columns_of(field, beside, lane):
    def at(k):
        return shifted(field, beside, k, lane)

    a1, b1, a2, b2 = at(1), at(-1), at(2), at(-2)
    slope_c = first(a1, b1, a2, b2)
    curve_cc = second(field, (a1 + b1, a2 + b2, at(3) + at(-3), at(4) + at(-4)))
    return slope_c, curve_cc


def column_slope(field, beside, lane):
    def at(k):
        return shifted(field, beside, k, lane)

    return first(at(1), at(-1), at(2), at(-2))


def near_kernel(blocks, p_ref, up_ref, down_ref, r_ref, c_ref, rr_ref, rc_ref, cc_ref, f_ref):
    lane = lanes_of(16)

    def rows(b, _):
        col = pl.multiple_of(b * LANES, LANES)
        base = pl.multiple_of(b * STRIDE, STRIDE)
        out = pl.multiple_of(b * 16, 16)
        window = f_ref.at[pl.ds(base, STRIDE), :]
        window[4:8, :] = up_ref[:, pl.ds(col, LANES)]
        window[8:24, :] = p_ref[:, pl.ds(col, LANES)]
        window[24:28, :] = down_ref[:, pl.ds(col, LANES)]
        slope, curve = rows_of(window)
        r_ref[pl.ds(out, 16), :] = slope
        rr_ref[pl.ds(out, 16), :] = curve
        return 0

    lax.fori_loop(0, blocks, rows, 0, unroll=8)

    def columns(b, _):
        before = lax.rem(b + (blocks - 1), blocks)
        after = lax.rem(b + 1, blocks)

        def of(i):
            return p_ref[:, pl.ds(pl.multiple_of(i * LANES, LANES), LANES)]

        def slope_of(i):
            return r_ref[pl.ds(pl.multiple_of(i * 16, 16), 16), :]

        far = lane >= LANES // 2
        slope_c, curve_cc = columns_of(of(b), jnp.where(far, of(before), of(after)), lane)
        curve_rc = column_slope(slope_of(b), jnp.where(far, slope_of(before), slope_of(after)), lane)
        out = pl.ds(pl.multiple_of(b * 16, 16), 16)
        c_ref[out, :] = slope_c
        rc_ref[out, :] = curve_rc
        cc_ref[out, :] = curve_cc
        return 0

    lax.fori_loop(0, blocks, columns, 0, unroll=8)


def near_fields(potentials, up, down):
    height, width = potentials.shape[1:]
    blocks = width // LANES
    shape = jax.ShapeDtypeStruct((blocks * 16, LANES), jnp.float32)
    return pl.pallas_call(
        functools.partial(near_kernel, blocks),
        grid=(1,),
        out_shape=(shape,) * 5,
        in_specs=[pl.BlockSpec((None, height, width), lambda i: (0, 0, 0)), VMEM, VMEM],
        out_specs=(VMEM,) * 5,
        scratch_shapes=[pltpu.VMEM((blocks * STRIDE, LANES), jnp.float32)],
        compiler_params=params(16),
        cost_estimate=pl.CostEstimate(flops=60_000_000, bytes_accessed=7_000_000, transcendentals=0),
        name="near_fields",
    )(potentials, up, down)


def index_kernel(blocks, caps, row_ref, col_ref, code_ref, level_ref):
    lane = lax.broadcasted_iota(jnp.int32, (RB, blocks), 1)
    row = row_ref[...]
    alike = lax.broadcasted_iota(jnp.int32, (RB, blocks), 0) == row
    count = alike.astype(jnp.int32)
    step = 1
    while step < blocks:
        count = count + jnp.where(lane >= step, pltpu.roll(count, step, 1), 0)
        step *= 2
    slot = jnp.sum(jnp.where(alike, count - 1, 0), axis=0, keepdims=True)
    source = lane[0:1] + col_ref[...]
    source = jnp.where(source >= blocks, source - blocks, source)
    code_ref[...] = source * 4096 + slot * 8 + row
    needed = jnp.max(count)
    level = jnp.int32(0)
    for cap in caps[:-1]:
        level = level + (needed > cap).astype(jnp.int32)
    level_ref[0] = level


def index_of(row_offset, col_offset, caps):
    blocks = row_offset.shape[0]
    code, level = pl.pallas_call(
        functools.partial(index_kernel, blocks, caps),
        out_shape=(jax.ShapeDtypeStruct((1, blocks), jnp.int32), jax.ShapeDtypeStruct((1,), jnp.int32)),
        in_specs=[VMEM, VMEM],
        out_specs=(VMEM, SMEM),
        name="block_index",
    )(row_offset.reshape(1, blocks), col_offset.reshape(1, blocks))
    return code.reshape(blocks), level[0]


def decoded(code):
    return code >> 12, (code >> 3) & 511, code & 7


def pack_kernel(blocks, cap, here_ref, code_ref, p_ref, out_ref):
    here = here_ref[0]
    tall = tiles_of(cap) * 8
    lane = lanes_of(8)
    far = lane >= LANES // 2

    def block(b, _):
        source, slot, shift = decoded(code_ref[b])
        start = ((here + RB - shift) & (RB - 1)) * tall
        before = jnp.where(source == 0, blocks - 1, source - 1)
        after = jnp.where(source == blocks - 1, 0, source + 1)

        def of(i):
            return p_ref[:, pl.ds(pl.multiple_of(i * LANES, LANES), LANES)]

        out_ref[pl.ds(pl.multiple_of(start + slot * 16, 8), 16), :] = of(source)
        left, right = of(before), of(after)
        place = (slot & 7) * EDGE
        row = pl.ds(pl.multiple_of(start + 16 * cap + (slot >> 3) * 8, 8), 8)
        for half in range(2):
            top = 8 * half
            edge = jnp.where(far, left[top : top + 8], right[top : top + 8])
            spot = place + half * (LANES // 2)
            moved = pltpu.roll(edge, spot + EDGE // 2, 1)
            mask = (lane >= spot) & (lane < spot + EDGE)
            pltpu.store(out_ref.at[row, :], moved, mask=mask)
        return 0

    lax.fori_loop(0, blocks, block, 0, unroll=8)


def pack(cap, here, code, potentials):
    height, width = potentials.shape[1:]
    blocks = width // LANES
    return pl.pallas_call(
        functools.partial(pack_kernel, blocks, cap),
        grid=(1,),
        out_shape=jax.ShapeDtypeStruct((RB * tiles_of(cap) * 8, LANES), jnp.float32),
        in_specs=[SMEM] * 2 + [pl.BlockSpec((None, height, width), lambda i: (1, 0, 0))],
        out_specs=VMEM,
        compiler_params=params(24),
        cost_estimate=pl.CostEstimate(flops=2_000_000, bytes_accessed=3_000_000, transcendentals=0),
        name="pack_blocks",
    )(here, code, potentials)


def unpack_kernel(blocks, cap, here_ref, code_ref, in_ref, w_ref, h_ref, head_ref, tail_ref):
    here = here_ref[0]
    tall = tiles_of(cap) * 8
    lane = lanes_of(8)

    def block(b, _):
        _, slot, shift = decoded(code_ref[b])
        start = ((here + shift) & (RB - 1)) * tall
        tile = in_ref[pl.ds(pl.multiple_of(start + slot * 16, 8), 16), :]
        col = pl.ds(pl.multiple_of(b * LANES, LANES), LANES)
        w_ref[pl.ds(pl.multiple_of(b * 16, 16), 16), :] = tile
        head_ref[:, col] = tile[0:4]
        tail_ref[:, col] = tile[12:16]
        edge = in_ref[pl.ds(pl.multiple_of(start + 16 * cap + (slot >> 3) * 8, 8), 8), :]
        spot = (b & 15) * EDGE
        turn = spot + LANES - (slot & 7) * EDGE
        mask = (lane >= spot) & (lane < spot + EDGE)
        row = pl.multiple_of((b >> 4) * 16, 16)
        pltpu.store(h_ref.at[pl.ds(row, 8), :], pltpu.roll(edge, turn & (LANES - 1), 1), mask=mask)
        half = (turn + LANES // 2) & (LANES - 1)
        pltpu.store(h_ref.at[pl.ds(row + 8, 8), :], pltpu.roll(edge, half, 1), mask=mask)
        return 0

    lax.fori_loop(0, blocks, block, 0, unroll=8)
    for g in range(blocks // 16):
        col = slice((blocks + g) * LANES, (blocks + g + 1) * LANES)
        head_ref[:, col] = h_ref[16 * g : 16 * g + 4, :]
        tail_ref[:, col] = h_ref[16 * g + 12 : 16 * g + 16, :]


def unpack(cap, blocks, here, code, arrived):
    ends = jax.ShapeDtypeStruct((4, (blocks + blocks // 16) * LANES), jnp.float32)
    return pl.pallas_call(
        functools.partial(unpack_kernel, blocks, cap),
        out_shape=(
            jax.ShapeDtypeStruct((blocks * 16, LANES), jnp.float32),
            jax.ShapeDtypeStruct((blocks, LANES), jnp.float32),
            ends,
            ends,
        ),
        in_specs=[SMEM] * 2 + [VMEM],
        out_specs=(VMEM,) * 4,
        compiler_params=params(24),
        cost_estimate=pl.CostEstimate(flops=2_000_000, bytes_accessed=3_000_000, transcendentals=0),
        name="unpack_blocks",
    )(here, code, arrived)


def edge_turn(b):
    return LANES - EDGE // 2 - b * EDGE


def columns_kernel(blocks, w_ref, h_ref, c_ref, cc_ref, g_ref):
    lane = lanes_of(16)

    def spread(i, _):
        edge = h_ref[pl.ds(pl.multiple_of(i * 16, 16), 16), :]
        for k in range(16):
            g_ref[pl.ds(pl.multiple_of(i * 256 + k * 16, 16), 16), :] = pltpu.roll(edge, edge_turn(k), 1)
        return 0

    lax.fori_loop(0, blocks // 16, spread, 0)

    def block(b, _):
        tile = pl.ds(pl.multiple_of(b * 16, 16), 16)
        c_ref[tile, :], cc_ref[tile, :] = columns_of(w_ref[tile, :], g_ref[tile, :], lane)
        return 0

    lax.fori_loop(0, blocks, block, 0, unroll=8)


def far_columns(windows, edges):
    blocks = edges.shape[0]
    return pl.pallas_call(
        functools.partial(columns_kernel, blocks),
        out_shape=(jax.ShapeDtypeStruct(windows.shape, jnp.float32),) * 2,
        in_specs=[VMEM, VMEM],
        out_specs=(VMEM, VMEM),
        scratch_shapes=[pltpu.VMEM(windows.shape, jnp.float32)],
        compiler_params=params(8),
        cost_estimate=pl.CostEstimate(flops=20_000_000, bytes_accessed=3_000_000, transcendentals=0),
        name="far_columns",
    )(windows, edges)


def far_kernel(
    ratio_ref, w_ref, h_ref, up_ref, down_ref, far_c_ref, far_cc_ref, r_ref, c_ref, rr_ref, rc_ref, cc_ref,
    conv_ref, shear_ref, rot_ref, disp_ref, f_ref, e_ref, s_ref,
):
    group = pl.program_id(0)
    blocks = h_ref.shape[0]
    lane = lanes_of(16)
    near_to_two, near_to_source, two_to_source = ratio_ref[0], ratio_ref[1], ratio_ref[2]
    half_one, half_two = 0.5 * near_to_source, 0.5 * two_to_source
    ends = pl.ds(pl.multiple_of((blocks + group) * LANES, LANES), LANES)
    e_ref[4:8, :] = up_ref[:, ends]
    e_ref[8:24, :] = h_ref[pl.ds(pl.multiple_of(group * 16, 16), 16), :]
    e_ref[24:28, :] = down_ref[:, ends]
    s_ref[...] = slope_rows(e_ref)

    def block(i, _):
        b = group * 16 + i
        col = pl.ds(pl.multiple_of(i * LANES, LANES), LANES)
        whole = pl.ds(pl.multiple_of(b * LANES, LANES), LANES)
        tile = pl.ds(pl.multiple_of(b * 16, 16), 16)
        window = f_ref.at[pl.ds(pl.multiple_of(i * STRIDE, STRIDE), STRIDE), :]
        window[4:8, :] = up_ref[:, whole]
        window[8:24, :] = w_ref[tile, :]
        window[24:28, :] = down_ref[:, whole]
        far_r, far_rr = rows_of(window)
        far_rc = column_slope(far_r, pltpu.roll(s_ref[...], edge_turn(i), 1), lane)
        far_cc = far_cc_ref[tile, :]
        near = pl.ds(pl.multiple_of(i * 16, 16), 16)
        near_rr, near_rc, near_cc = rr_ref[near, :], rc_ref[near, :], cc_ref[near, :]
        inner_rr = 1.0 - near_to_two * near_rr
        inner_rc = -near_to_two * near_rc
        inner_cc = 1.0 - near_to_two * near_cc
        chain_rr = far_rr * inner_rr + far_rc * inner_rc
        chain_rc = far_rr * inner_rc + far_rc * inner_cc
        chain_cr = far_rc * inner_rr + far_cc * inner_rc
        chain_cc = far_rc * inner_rc + far_cc * inner_cc
        conv_ref[:, col] = half_one * (near_rr + near_cc) + half_two * (chain_rr + chain_cc)
        shear_ref[0, :, col] = half_one * (near_cc - near_rr) + half_two * (chain_cc - chain_rr)
        shear_ref[1, :, col] = near_to_source * near_rc + half_two * (chain_rc + chain_cr)
        rot_ref[:, col] = half_two * (chain_cr - chain_rc)
        disp_ref[0, :, col] = near_to_source * r_ref[near, :] + two_to_source * far_r
        disp_ref[1, :, col] = near_to_source * c_ref[near, :] + two_to_source * far_c_ref[tile, :]
        return 0

    lax.fori_loop(0, 16, block, 0, unroll=16)


def assemble(ratios, windows, edges, above, below, far, near):
    blocks = edges.shape[0]
    wide = 16 * LANES
    flat = jax.ShapeDtypeStruct((16, blocks * LANES), jnp.float32)
    pair = jax.ShapeDtypeStruct((2, 16, blocks * LANES), jnp.float32)
    flat_spec = pl.BlockSpec((16, wide), lambda i: (0, i))
    pair_spec = pl.BlockSpec((2, 16, wide), lambda i: (0, 0, i))
    return pl.pallas_call(
        far_kernel,
        grid=(blocks // 16,),
        out_shape=(flat, pair, flat, pair),
        in_specs=[SMEM] + [VMEM] * 6 + [pl.BlockSpec((256, LANES), lambda i: (i, 0))] * 5,
        out_specs=(flat_spec, pair_spec, flat_spec, pair_spec),
        scratch_shapes=[
            pltpu.VMEM((16 * STRIDE, LANES), jnp.float32),
            pltpu.VMEM((STRIDE, LANES), jnp.float32),
            pltpu.VMEM((16, LANES), jnp.float32),
        ],
        compiler_params=params(16),
        cost_estimate=pl.CostEstimate(flops=40_000_000, bytes_accessed=6_000_000, transcendentals=0),
        name="far_fields",
    )(ratios, windows, edges, above, below, *far, *near)


def passed(x, by):
    size = lax.axis_size("row")
    return lax.ppermute(x, "row", [(i, (i + by) % size) for i in range(size)])


def near_plane(potentials):
    height = potentials.shape[1]
    above = passed(potentials[0, height - 4 :, :], 1)
    below = passed(potentials[0, :4, :], -1)
    return near_fields(potentials, above, below)


def near_blank(potentials):
    width = potentials.shape[2]
    return (jnp.zeros((width // LANES * 16, LANES), jnp.float32),) * 5


def exchange(cap, groups, potentials, here, code):
    blocks = potentials.shape[2] // LANES
    packed = pack(cap, here, code, potentials).reshape(RB, tiles_of(cap) * 8, LANES)
    arrived = lax.all_to_all(packed, "row", 0, 0, axis_index_groups=groups)
    near = lax.cond(here[0] >= 0, near_plane, near_blank, potentials)
    arrived = arrived.reshape(RB * tiles_of(cap) * 8, LANES)
    return unpack(cap, blocks, here, code, arrived), near


def per_device(potentials, ratios, row_offset, col_offset):
    stride = lax.axis_size("row") // RB
    blocks = potentials.shape[2] // LANES
    caps = tuple(c for c in CAPS if c < blocks) + (blocks,)
    code, level = index_of(row_offset, col_offset, caps)
    here = (lax.axis_index("row") // stride).astype(jnp.int32).reshape(1)
    groups = [[y * stride + j for y in range(RB)] for j in range(stride)]
    (windows, edges, heads, tails), near = lax.switch(
        level,
        [functools.partial(exchange, cap, groups) for cap in caps],
        potentials, here, code,
    )
    above = passed(tails, 1)
    below = passed(heads, -1)
    far = far_columns(windows, edges)
    return assemble(ratios, windows, edges, above, below, far, near)


def solution(mesh):
    return jax.shard_map(
        per_device,
        mesh=mesh,
        in_specs=(P("cosmo", "row", None), P("cosmo"), P("cosmo"), P("cosmo")),
        out_specs=(
            P(("cosmo", "row"), None),
            P(None, ("cosmo", "row"), None),
            P(("cosmo", "row"), None),
            P(None, ("cosmo", "row"), None),
        ),
        check_vma=False,
    )
```

time: 104 us -> 86.1 us (0.83)
  the two profiles are of different devices: /device:TPU:527 before, /device:TPU:519 now
where the time goes in v2:
time: 86.1 us; the launch traced here: 87.2 us
  Pallas kernels  33.9 us (39%)
  waiting for transfers between devices  30.9 us (36%)
  starting transfers between devices  19.3 us (22%)
  between operations  1.53 us (2%)
  local copies, waits for them, and re-layouts  1.3 us (2%)
    all_to_all x1, waiting for transfers between devices, exchange(): arrived = lax.all_to_all(packed, 'row', 0, 0, axis_index_groups=groups)  21.6 us
    all_to_all x1, starting transfers between devices, exchange(): arrived = lax.all_to_all(packed, 'row', 0, 0, axis_index_groups=groups)  12.9 us
    pallas_call x1, Pallas kernels, assemble(): pl.pallas_call(far_kernel, grid=(blocks // 16,), out_shape=(flat, pair, f...  9.52 us
    ppermute x4, waiting for transfers between devices, passed(): return lax.ppermute(x, 'row', [(i, (i + by) % size) for i in range(size)])  9.29 us
    pallas_call x1, Pallas kernels, near_fields(): pl.pallas_call(functools.partial(near_kernel, blocks), grid=(1,), out_sha...  8.88 us
    ppermute x4, starting transfers between devices, passed(): return lax.ppermute(x, 'row', [(i, (i + by) % size) for i in range(size)])  6.38 us
    pallas_call x1, Pallas kernels, far_columns(): pl.pallas_call(functools.partial(columns_kernel, blocks), out_shape=(jax....  5.38 us
    pallas_call x1, Pallas kernels, pack(): pl.pallas_call(functools.partial(pack_kernel, blocks, cap), grid=(1,), ou...  4.73 us
  transfers between devices with their start and end apart: 5, of which 4 were waited for; matrix products, arithmetic and copies ran while one was open for 1% of the time, Pallas kernels for 16%

profile of v2, /device:TPU:519, one launch (start us, length us, event | category | flops | bytes accessed | tf_op | source)
XLA Modules:
  0.0 87.2 jit_solution(11410254729582246230)
XLA Ops:
  0.6 1.9 %block_index.1 = (s32[1,128]{1,0:T(1,128)S(1)}, s32[1]{0:T(128)}) custom-call(s32[1,128]{1,0:T(1,128)} %bitcast.78, s32[1,128]{1,0:T(1,128)} %bitcast.79), custom_call_target="tpu_custom_call" | custom-call | tf_op jit(solution)/shard_map/block_index/pallas_call | solution.py:160
  3.2 0.0 copy-start.2
  3.2 63.9 %conditional.10 = (f32[2048,128]{1,0:T(8,128)}, f32[128,128]{1,0:T(8,128)}, f32[4,17408]{1,0:T(4,128)}, f32[4,17408]{1,0:T(4,128)}, f32[2048,128]{1,0:T(8,128)},...) conditional(s32[]{:T(128)} %bitcast.38, (s32[1]{0:T(128)}, ...), branch_computations={%region_0.3_spmd, %region_3.6_spmd, %region_6.9_spmd, %region_9.12... | conditional | flops 64000000 | bytes 86924872 | solution.py:409
  3.4 4.7 %pack_blocks.14 = f32[3264,128]{1,0:T(8,128)} custom-call(s32[1]{0:T(128)} %get-tuple-element.146.here_ref, s32[128]{0:T(128)S(1)} %get-tuple-element.147.code_ref, f32[2,16,16384]{2,1,0:T(8,128)} %get-tuple-element.148.p_ref), custom_call_target="tpu_custom_call" | custom-call | flops 2000000 | bytes 3000000 | tf_op jit(solution)/shard_map/cond/branch_5_fun/pack_blocks/pallas_call | solution.py:208
  8.1 12.9 %all-to-all-start.5 = ((f32[8,408,128]{2,1,0:T(8,128)}), f32[8,408,128]{2,1,0:T(8,128)S(1)}, u32[]{:S(2)}, u32[]{:S(2)}) async-start(f32[8,408,128]{2,1,0:T(8,128)} %bitcast.22), calls=%async_computation.5 | async-start | bytes 3342336 | tf_op jit(solution)/shard_map/cond/branch_5_fun/all_to_all | solution.py:396
  21.0 20.9 %conditional.5 = ((f32[2048,128]{1,0:T(8,128)}, f32[2048,128]{1,0:T(8,128)}, f32[2048,128]{1,0:T(8,128)}, f32[2048,128]{1,0:T(8,128)}, f32[2048,128]{1,0:T(8,128)})) conditional(s32[]{:T(128)} %convert_element_type.23, () %tuple.85, f32[2,16,16384]{2,1,0:T(8,128)} %get-tuple-element.148.p_ref), branch_computations={%region_16.16_spmd, %region_17.17_spmd} | conditional | flops 60000000 | bytes 10145816 | solution.py:397
  21.0 1.3 %slice_bitcast_fusion.10 = (f32[4,16384]{1,0:T(4,128)S(1)}, f32[4,16384]{1,0:T(4,128)S(1)}) fusion(f32[2,16,16384]{2,1,0:T(8,128)} %p_ref.5), kind=kLoop, calls=%fused_computation.10 | loop fusion | bytes 1048576 | tf_op jit(solution)/shard_map/cond/branch_5_fun/cond/branch_1_fun/squeeze | solution.py:384
  22.3 3.4 %collective-permute-start.10 = (f32[4,16384]{1,0:T(4,128)S(1)}, f32[4,16384]{1,0:T(4,128)S(1)}, u32[]{:S(2)}, u32[]{:S(2)}) collective-permute-start(f32[4,16384]{1,0:T(4,128)S(1)} %get-tuple-element.239), channel_id=1, source_target_pairs={{0,1},{1,2},{2,3},{3,4},{4,5},{5,6},{6,7},{7,8},{8,9},{9,10},{10,1... | collective-permute-start | bytes 786440 | tf_op jit(solution)/shard_map/cond/branch_5_fun/cond/branch_1_fun/ppermute | solution.py:378
  25.8 0.0 collective-permute-start.11
  25.8 3.3 %collective-permute-done.10.up_ref = f32[4,16384]{1,0:T(4,128)S(1)} collective-permute-done((f32[4,16384]{1,0:T(4,128)S(1)}, f32[4,16384]{1,0:T(4,128)S(1)}, u32[]{:S(2)}, u32[]{:S(2)}) %collective-permute-start.10) | collective-permute-done | bytes 262176 | tf_op jit(solution)/shard_map/cond/branch_5_fun/cond/branch_1_fun/ppermute | solution.py:378
  29.1 4.0 %collective-permute-done.11.down_ref = f32[4,16384]{1,0:T(4,128)S(1)} collective-permute-done((f32[4,16384]{1,0:T(4,128)S(1)}, f32[4,16384]{1,0:T(4,128)S(1)}, u32[]{:S(2)}, u32[]{:S(2)}) %collective-permute-start.11) | collective-permute-done | bytes 262176 | tf_op jit(solution)/shard_map/cond/branch_5_fun/cond/branch_1_fun/ppermute | solution.py:378
  33.1 8.9 %near_fields.14 = (f32[2048,128]{1,0:T(8,128)}, f32[2048,128]{1,0:T(8,128)}, f32[2048,128]{1,0:T(8,128)}, f32[2048,128]{1,0:T(8,128)}, f32[2048,128]{1,0:T(8,128)}) custom-call(f32[2,16,16384]{2,1,0:T(8,128)} %p_ref.5, f32[4,16384]{1,0:T(4,128)S(1)} %collective-permute-done.10.up_ref, f32[4,16384]{1,0:T(4,128)S(1)} %collective-permute-done.11.down_ref), custom_call_target="tpu_custom_call" | custom-call | flops 60000000 | bytes 7000000 | tf_op jit(solution)/shard_map/cond/branch_5_fun/cond/branch_1_fun/near_fields/pallas_call | solution.py:125
  41.9 21.6 %all-to-all-done.5 = f32[8,408,128]{2,1,0:T(8,128)S(1)} async-done(((f32[8,408,128]{2,1,0:T(8,128)}), f32[8,408,128]{2,1,0:T(8,128)S(1)}, u32[]{:S(2)}, u32[]{:S(2)}) %all-to-all-start.5) | async-done | bytes 1671200 | tf_op jit(solution)/shard_map/cond/branch_5_fun/all_to_all | solution.py:396
  63.6 3.5 %unpack_blocks.14 = (f32[2048,128]{1,0:T(8,128)}, f32[128,128]{1,0:T(8,128)}, f32[4,17408]{1,0:T(4,128)}, f32[4,17408]{1,0:T(4,128)}) custom-call(s32[1]{0:T(128)} %get-tuple-element.146.here_ref, s32[128]{0:T(128)S(1)} %get-tuple-element.147.code_ref, f32[3264,128]{1,0:T(8,128)S(1)} %bitcast.63), custom_call_target="tpu_custom_call" | custom-call | flops 2000000 | bytes 3000000 | tf_op jit(solution)/shard_map/cond/branch_5_fun/unpack_blocks/pallas_call | solution.py:252
  67.1 2.9 %collective-permute-start.18 = (f32[4,17408]{1,0:T(4,128)}, f32[4,17408]{1,0:T(4,128)S(1)}, u32[]{:S(2)}, u32[]{:S(2)}) collective-permute-start(f32[4,17408]{1,0:T(4,128)} %get-tuple-element.219), channel_id=1, source_target_pairs={{0,1},{1,2},{2,3},{3,4},{4,5},{5,6},{6,7},{7,8},{8,9},{9,10},{10,1... | collective-permute-start | bytes 835592 | tf_op jit(solution)/shard_map/ppermute | solution.py:378
  70.0 0.0 collective-permute-start.19
  70.0 5.4 %far_columns.1 = (f32[2048,128]{1,0:T(8,128)S(1)}, f32[2048,128]{1,0:T(8,128)S(1)}) custom-call(f32[2048,128]{1,0:T(8,128)} %get-tuple-element.217.w_ref, f32[128,128]{1,0:T(8,128)} %get-tuple-element.218.h_ref), custom_call_target="tpu_custom_call" | custom-call | flops 20000000 | bytes 3000000 | tf_op jit(solution)/shard_map/far_columns/pallas_call | solution.py:293
  75.4 0.0 collective-permute-done.18.up_ref
  75.4 2.0 %collective-permute-done.19.down_ref = f32[4,17408]{1,0:T(4,128)S(1)} collective-permute-done((f32[4,17408]{1,0:T(4,128)}, f32[4,17408]{1,0:T(4,128)S(1)}, u32[]{:S(2)}, u32[]{:S(2)}) %collective-permute-start.19) | collective-permute-done | bytes 278560 | tf_op jit(solution)/shard_map/ppermute | solution.py:378
  77.4 0.0 copy-done.2
  77.4 9.5 %far_fields.1 = (f32[16,16384]{1,0:T(8,128)}, f32[2,16,16384]{2,1,0:T(8,128)}, f32[16,16384]{1,0:T(8,128)}, f32[2,16,16384]{2,1,0:T(8,128)}) custom-call(f32[3]{0:T(128)S(1)} %copy-done.2, f32[2048,128]{1,0:T(8,128)} %get-tuple-element.217.w_ref, f32[128,128]{1,0:T(8,128)} %get-tuple-element.218.h_ref, f32[4,17408]{1,0:T(4,128)S(1)} %collective-permute-done.18.up_ref, ...), custom_call_target="tpu_custom_call" | custom-call | flops 40000000 | bytes 6000000 | tf_op jit(solution)/shard_map/far_fields/pallas_call | solution.py:359
Async XLA Ops:
  3.2 74.3 %copy-start.2 = (f32[3]{0:T(128)S(1)}, f32[3]{0:T(128)}, u32[]{:S(2)}) copy-start(f32[3]{0:T(128)} %ratio_ref.1) | copy-start | bytes 40
  8.1 55.4 %all-to-all-start.5 = ((f32[8,408,128]{2,1,0:T(8,128)}), f32[8,408,128]{2,1,0:T(8,128)S(1)}, u32[]{:S(2)}, u32[]{:S(2)}) async-start(f32[8,408,128]{2,1,0:T(8,128)} %bitcast.22), calls=%async_computation.5 | async-start | bytes 3342336 | tf_op jit(solution)/shard_map/cond/branch_5_fun/all_to_all | solution.py:396
  22.3 6.8 %collective-permute-start.10 = (f32[4,16384]{1,0:T(4,128)S(1)}, f32[4,16384]{1,0:T(4,128)S(1)}, u32[]{:S(2)}, u32[]{:S(2)}) collective-permute-start(f32[4,16384]{1,0:T(4,128)S(1)} %get-tuple-element.239), channel_id=1, source_target_pairs={{0,1},{1,2},{2,3},{3,4},{4,5},{5,6},{6,7},{7,8},{8,9},{9,10},{10,1... | collective-permute-start | bytes 786440 | tf_op jit(solution)/shard_map/cond/branch_5_fun/cond/branch_1_fun/ppermute | solution.py:378
  25.8 7.3 %collective-permute-start.11 = (f32[4,16384]{1,0:T(4,128)S(1)}, f32[4,16384]{1,0:T(4,128)S(1)}, u32[]{:S(2)}, u32[]{:S(2)}) collective-permute-start(f32[4,16384]{1,0:T(4,128)S(1)} %get-tuple-element.238), channel_id=1, source_target_pairs={{0,127},{1,0},{2,1},{3,2},{4,3},{5,4},{6,5},{7,6},{8,7},{9,8},{10,... | collective-permute-start | bytes 786440 | tf_op jit(solution)/shard_map/cond/branch_5_fun/cond/branch_1_fun/ppermute | solution.py:378
  67.1 8.3 %collective-permute-start.18 = (f32[4,17408]{1,0:T(4,128)}, f32[4,17408]{1,0:T(4,128)S(1)}, u32[]{:S(2)}, u32[]{:S(2)}) collective-permute-start(f32[4,17408]{1,0:T(4,128)} %get-tuple-element.219), channel_id=1, source_target_pairs={{0,1},{1,2},{2,3},{3,4},{4,5},{5,6},{6,7},{7,8},{8,9},{9,10},{10,1... | collective-permute-start | bytes 835592 | tf_op jit(solution)/shard_map/ppermute | solution.py:378
  70.0 7.4 %collective-permute-start.19 = (f32[4,17408]{1,0:T(4,128)}, f32[4,17408]{1,0:T(4,128)S(1)}, u32[]{:S(2)}, u32[]{:S(2)}) collective-permute-start(f32[4,17408]{1,0:T(4,128)} %get-tuple-element.220), channel_id=1, source_target_pairs={{0,127},{1,0},{2,1},{3,2},{4,3},{5,4},{6,5},{7,6},{8,7},{9,8},{10,... | collective-permute-start | bytes 835592 | tf_op jit(solution)/shard_map/ppermute | solution.py:378
